TPU v7x, 256 devices: a whole 4x4x8 slice. The times are simulated.
256 devices in a mesh: dp: 32 (over y, x, core), mp: 8 (over z).
Axes of the slice: x: 4, y: 4, z: 8, core: 2. Of those that a mesh axis runs over, the one named last changes fastest.
Arguments:
- clean: bfloat16 [128, 256, 1536], P('dp', None, 'mp'), may hold values from -6 to 6
- noise: bfloat16 [128, 256, 1536], P('dp', None, 'mp'), may hold values from -6 to 6
- teacher_first: bfloat16 [128, 256, 1536], P('dp', None, 'mp'), may hold values from -6 to 6
- teacher_second: bfloat16 [128, 256, 1536], P('dp', None, 'mp'), may hold values from -6 to 6
- step_index: int32 [128], P('dp'), may hold values from 8 to 32
- teacher_count: int32 [128], P('dp'), may hold values from 64 to 256
- up_master: float32 [1536, 6144], P('dp', 'mp'), may hold values from -6 to 6
- down_master: float32 [1536, 6144], P('dp', 'mp'), may hold values from -6 to 6
- up_moment: float32 [1536, 6144], P('dp', 'mp'), may hold values from -1.8 to 1.8
- down_moment: float32 [1536, 6144], P('dp', 'mp'), may hold values from -1.8 to 1.8
- up_second: float32 [1536, 6144], P('dp', 'mp'), may hold values from 0.002 to 0.032
- down_second: float32 [1536, 6144], P('dp', 'mp'), may hold values from 0.002 to 0.032
Outputs:
- new_up_master: float32 [1536, 6144], P('dp', 'mp')
- new_down_master: float32 [1536, 6144], P('dp', 'mp')
- new_up_moment: float32 [1536, 6144], P('dp', 'mp')
- new_down_moment: float32 [1536, 6144], P('dp', 'mp')
- new_up_second: float32 [1536, 6144], P('dp', 'mp')
- new_down_second: float32 [1536, 6144], P('dp', 'mp')
- loss_mean: float32 [], replicated
Inputs may be any that keep to these rules, and one draw needn't show every extreme that they name: `step_index`: student step k with 2k at most the sample's teacher_count.
All inputs are finite; a program needn't handle non-finite values.
Results may differ from a plain program's by a relative error of at most 0.002.
Values may be sent and summed in bfloat16 or wider, within the bound.
No kernel may reach another device: no remote copies, remote signals or barrier semaphores. Data moves between devices by JAX's collectives and lax.ppermute only.
A program may use at most 64 MiB of HBM per device.

v0:
```python
import functools
import math
import jax
import jax.numpy as jnp
from jax import lax
from jax.sharding import Mesh
from jax.sharding import PartitionSpec as P

DP = ("dp_0", "dp_1", "dp_2")
DP_MP = ("dp_0", "dp_1", "dp_2", "mp")
adam_count = 100.0
learn_rate = 0.05
decay_rate = 0.01


def sent_together(arrays, axis, dim, along):
    both = jnp.concatenate(arrays, axis=along)
    result, at, outs = (lax.all_gather(both, axis, axis=dim, tiled=True), 0, [])
    for a in arrays:
        outs.append(lax.slice_in_dim(result, at, at + a.shape[along], axis=along))
        at += a.shape[along]
    return tuple(outs)


def sent_together_2(arrays, axis, dim, along):
    ends, at = ([], 0)
    for a in arrays[:-1]:
        at += a.shape[along]
        ends.append(at)
    both = jnp.concatenate(arrays, axis=along)
    return tuple(
        jnp.split(lax.psum_scatter(both, axis, scatter_dimension=dim, tiled=True), ends, axis=along)
    )


def by_axis(shard, axes):
    return functools.reduce(lax.psum, axes, shard)


def gelu_pair(preact):
    tanh_arg = 0.7978845608028654 * (preact + 0.044715 * preact * preact * preact)
    tanh_val = jnp.tanh(tanh_arg)
    activation = 0.5 * preact * (1.0 + tanh_val)
    slopes = 0.5 * (1.0 + tanh_val) + 0.5 * preact * (
        1.0 - tanh_val * tanh_val
    ) * 0.7978845608028654 * (1.0 + 3.0 * 0.044715 * preact * preact)
    return (activation, slopes)


def distill_target(clean, noise, teacher_first, teacher_second, step_index, teacher_count):
    steps_float = teacher_count.astype(jnp.float32)[:, None, None]
    doubled = 2.0 * step_index.astype(jnp.float32)[:, None, None]
    quarter_turn = 0.5 * math.pi
    time_now = doubled / steps_float
    time_mid = (doubled - 1.0) / steps_float
    time_end = (doubled - 2.0) / steps_float
    alpha_now = jnp.cos(quarter_turn * time_now)
    sigma_now = jnp.sin(quarter_turn * time_now)
    alpha_mid = jnp.cos(quarter_turn * time_mid)
    sigma_mid = jnp.sin(quarter_turn * time_mid)
    alpha_end = jnp.cos(quarter_turn * time_end)
    sigma_end = jnp.sin(quarter_turn * time_end)
    first_f = teacher_first.astype(jnp.float32)
    second_f = teacher_second.astype(jnp.float32)
    latent_now = alpha_now * clean.astype(jnp.float32) + sigma_now * noise.astype(jnp.float32)
    noise_now = (latent_now - alpha_now * first_f) / sigma_now
    latent_mid = alpha_mid * first_f + sigma_mid * noise_now
    noise_mid = (latent_mid - alpha_mid * second_f) / sigma_mid
    latent_end = alpha_end * second_f + sigma_end * noise_mid
    sigma_ratio = sigma_end / sigma_now
    target = (latent_end - sigma_ratio * latent_now) / (alpha_end - sigma_ratio * alpha_now)
    weighting = jnp.maximum(alpha_now * alpha_now / (sigma_now * sigma_now), 1.0)[:, 0, 0]
    return (latent_now, target, weighting)


def adam_update(master, moment, second, gradient, factor):
    clipped = gradient * factor
    moment_new = 0.9 * moment + 0.1 * clipped
    second_new = 0.999 * second + 0.001 * clipped * clipped
    first_hat = moment_new / (1.0 - 0.9**adam_count)
    second_hat = second_new / (1.0 - 0.999**adam_count)
    master_new = master - learn_rate * (
        first_hat / (jnp.sqrt(second_hat) + 1e-08) + decay_rate * master
    )
    return (master_new, moment_new, second_new)


def per_device(
    clean,
    noise,
    teacher_first,
    teacher_second,
    step_index,
    teacher_count,
    up_master,
    down_master,
    up_moment,
    down_moment,
    up_second,
    down_second,
):
    samples_dev, token_count, width_local = clean.shape
    sample_total = samples_dev * lax.axis_size(DP)
    row_count = samples_dev * token_count
    latent, target, weighting = distill_target(
        clean, noise, teacher_first, teacher_second, step_index, teacher_count
    )
    noisy_rows = latent.reshape(row_count, width_local).astype(jnp.bfloat16)
    gathered = lax.all_gather(noisy_rows, "mp", axis=1, tiled=True)
    gathered_f = gathered.astype(jnp.float32)
    normed = (
        gathered_f * lax.rsqrt(jnp.mean(gathered_f * gathered_f, axis=1, keepdims=True) + 1e-06)
    ).astype(jnp.bfloat16)
    up_full, down_full = sent_together(
        (up_master.astype(jnp.bfloat16), down_master.astype(jnp.bfloat16)), DP, 0, 1
    )
    width_full = up_full.shape[0]
    hidden_local = up_full.shape[1]
    dscale = width_full ** (-0.5)
    fscale = (hidden_local * lax.axis_size("mp")) ** (-0.5)
    preact = jnp.dot(normed, up_full, preferred_element_type=jnp.float32) * dscale
    activation, slopes = gelu_pair(preact)
    hidden = activation.astype(jnp.bfloat16)
    partial_value = (
        lax.dot_general(
            hidden, down_full, (((1,), (1,)), ((), ())), preferred_element_type=jnp.float32
        )
        * fscale
    )
    branch = lax.psum_scatter(
        partial_value.astype(jnp.bfloat16), "mp", scatter_dimension=1, tiled=True
    ).astype(jnp.float32)
    errors = latent + branch.reshape(latent.shape) - target
    weight_cube = weighting[:, None, None]
    loss_part = jnp.sum(weight_cube * errors * errors)
    dpred = (
        (2.0 * weight_cube / sample_total * errors)
        .astype(jnp.bfloat16)
        .reshape(row_count, width_local)
    )
    piece = lax.all_gather(dpred, "mp", axis=1, tiled=True)
    summed = jnp.dot(piece, down_full, preferred_element_type=jnp.float32)
    grad_piece = (
        lax.dot_general(piece, hidden, (((0,), (0,)), ((), ())), preferred_element_type=jnp.float32)
        * fscale
    )
    dpre = (summed * fscale * slopes).astype(jnp.bfloat16)
    grad_up = (
        lax.dot_general(normed, dpre, (((0,), (0,)), ((), ())), preferred_element_type=jnp.float32)
        * dscale
    )
    owned_up, owned_down = sent_together_2((grad_up, grad_piece), DP, 0, 1)
    squares = jnp.sum(owned_up * owned_up) + jnp.sum(owned_down * owned_down)
    loss_total, square_total = (by_axis(loss_part, DP_MP), by_axis(squares, DP_MP))
    clip_limit = math.sqrt(2.0 * width_full * hidden_local * lax.axis_size("mp"))
    factor = clip_limit / jnp.maximum(jnp.sqrt(square_total), clip_limit)
    new_up, up_m, up_v = adam_update(up_master, up_moment, up_second, owned_up, factor)
    new_down, down_m, down_v = adam_update(
        down_master, down_moment, down_second, owned_down, factor
    )
    loss_mean = loss_total / (sample_total * token_count * width_full)
    return (new_up, new_down, up_m, down_m, up_v, down_v, loss_mean)


def solution(mesh):
    split = Mesh(mesh.devices.reshape(4, 4, 2, mesh.shape["mp"]), ("dp_0", "dp_1", "dp_2", "mp"))
    placed = (
        P(DP, None, "mp"),
        P(DP, None, "mp"),
        P(DP, None, "mp"),
        P(DP, None, "mp"),
        P(DP),
        P(DP),
        P(DP, "mp"),
        P(DP, "mp"),
        P(DP, "mp"),
        P(DP, "mp"),
        P(DP, "mp"),
        P(DP, "mp"),
    )
    return jax.shard_map(
        per_device,
        mesh=split,
        in_specs=placed,
        out_specs=(
            P(DP, "mp"),
            P(DP, "mp"),
            P(DP, "mp"),
            P(DP, "mp"),
            P(DP, "mp"),
            P(DP, "mp"),
            P(),
        ),
        check_vma=False,
    )
```

profile of v0, /device:TPU:2, one launch (start us, length us, event | category | flops | bytes accessed | tf_op | source)
XLA Modules:
  0.0 404.3 jit_solution(1169654670336712328)
XLA Ops:
  8.0 1.3 fusion.27
  10.2 0.9 convert_element_type.57
  12.8 45.4 %all-gather.4.cloned.1.call-done = bf16[1024,1536]{0,1:T(8,128)(2,1)} async-done(((bf16[1024,192]{0,1:T(8,128)(2,1)}), bf16[1024,1536]{0,1:T(8,128)(2,1)}) %all-gather.4.cloned.1.call-update) | async-done | bytes 3145744 | tf_op jit(solution)/shard_map/all_gather | solution.py:109
  58.3 2.7 fusion
  61.0 50.3 %all-gather.6.cloned.1.call-done = bf16[1536,1536]{1,0:T(8,128)(2,1)} async-done(((bf16[48,1536]{1,0:T(8,128)(2,1)}), bf16[1536,1536]{1,0:T(8,128)(2,1)}) %all-gather.6.cloned.1.call-update) | async-done | bytes 4718608 | tf_op jit(solution)/shard_map/all_gather | solution.py:18
  111.3 4.6 %fusion.6 = f32[1024,768]{1,0:T(8,128)S(1)} fusion(bf16[1024,1536]{0,1:T(8,128)(2,1)S(1)} %copy-done, f32[1024]{0:T(1024)S(1)} %add_rsqrt_fusion, bf16[1536,1536]{1,0:T(8,128)(2,1)} %all-gather.6.cloned.1.call-done), kind=kOutput, calls=%fused_computation.14 | convolution fusion | flops 2420637696 | bytes 8654848 | tf_op jit(solution)/shard_map/dot_general | solution.py:121
  115.9 1.8 copy-done.14
  117.7 4.4 %multiply_convert_fusion = bf16[1024,1536]{0,1:T(8,128)(2,1)} fusion(bf16[1536,1536]{1,0:T(8,128)(2,1)S(1)} %copy-done.12, f32[1024,768]{1,0:T(8,128)S(1)} %fusion.6), kind=kOutput, calls=%fused_computation.5 | convolution fusion | flops 2426929152 | bytes 8650752 | tf_op jit(solution)/shard_map/dot_general | solution.py:125
  122.2 46.7 %reduce-scatter.5.cloned.1.call-done = bf16[1024,192]{0,1:T(8,128)(2,1)} async-done(((bf16[1024,1536]{0,1:T(8,128)(2,1)}), bf16[1024,192]{0,1:T(8,128)(2,1)}) %reduce-scatter.5.cloned.1.call-update) | async-done | bytes 393232 | tf_op jit(solution)/shard_map/reduce_scatter | solution.py:130
  169.0 1.1 reshape.70
  170.1 1.5 fusion.25
  172.8 44.4 %all-gather.8.cloned.1.call-done = bf16[1024,1536]{0,1:T(8,128)(2,1)} async-done(((bf16[1024,192]{0,1:T(8,128)(2,1)}), bf16[1024,1536]{0,1:T(8,128)(2,1)}) %all-gather.8.cloned.1.call-update) | async-done | bytes 3145744 | tf_op jit(solution)/shard_map/all_gather | solution.py:141
  217.2 8.1 %multiply_convert_fusion.1 = bf16[1024,768]{1,0:T(8,128)(2,1)S(1)} fusion(f32[1024,768]{1,0:T(8,128)} %copy-done.14, bf16[1024,1536]{0,1:T(8,128)(2,1)} %all-gather.8.cloned.1.call-done, bf16[1536,1536]{1,0:T(8,128)(2,1)} %all-gather.6.cloned.1.call-done), kind=kOutput, calls=%fused_computation.11 | convolution fusion | flops 2432434176 | bytes 10223616 | tf_op jit(solution)/shard_map/dot_general | solution.py:142
  225.3 5.2 %convolution_multiply_fusion = f32[1536,768]{0,1:T(8,128)S(1)} fusion(bf16[1024,1536]{0,1:T(8,128)(2,1)S(1)} %copy-done.13, f32[1024,768]{1,0:T(8,128)} %copy-done.14), kind=kOutput, calls=%fused_computation.7 | convolution fusion | flops 2424963072 | bytes 11010048 | tf_op jit(solution)/shard_map/dot_general | solution.py:144
  230.5 2.8 convolution_multiply_fusion.1
  233.3 4.5 %pad_maximum_fusion = f32[1536,1536]{0,1:T(8,128)} fusion(f32[1536,768]{0,1:T(8,128)S(1)} %convolution_multiply_fusion, f32[1536,768]{0,1:T(8,128)S(1)} %convolution_multiply_fusion.1), kind=kLoop, calls=%fused_computation | loop fusion | flops 2359296 | bytes 18874368 | tf_op jit(solution)/shard_map/concatenate | solution.py:30
  237.8 9.6 %copy.73 = f32[1536,1536]{1,0:T(8,128)} copy(f32[1536,1536]{0,1:T(8,128)} %pad_maximum_fusion) | data formatting | bytes 18874368
  247.5 101.6 %reduce-scatter.7.cloned.1.call-done = f32[48,1536]{1,0:T(8,128)} async-done(((f32[1536,1536]{1,0:T(8,128)}), f32[48,1536]{1,0:T(8,128)}) %reduce-scatter.7.cloned.1.call-update) | async-done | bytes 294928 | tf_op jit(solution)/shard_map/reduce_scatter | solution.py:32
  349.1 1.6 multiply_reduce_fusion
  352.0 9.9 %all-reduce.2 = (f32[]{:T(128)}, f32[]{:T(128)}) all-reduce(f32[]{:T(128)S(6)} %add.97, f32[]{:T(128)} %get-tuple-element.44), channel_id=1, replica_groups=mesh['dp_0'=4,'dp_1'=4,'dp_2'=2,'mp'=8] {'dp_0'}, use_global_device_ids=true, to_apply=%region_5.0 | all-reduce | flops 2 | bytes 16 | tf_op jit(solution)/shard_map/psum | solution.py:37
  361.9 10.1 %all-reduce.1 = (f32[]{:T(128)}, f32[]{:T(128)}) all-reduce(f32[]{:T(128)} %get-tuple-element.34, f32[]{:T(128)} %get-tuple-element.35), channel_id=1, replica_groups=mesh['dp_0'=4,'dp_1'=4,'dp_2'=2,'mp'=8] {'dp_1'}, use_global_device_ids=true, to_apply=%region_6.0 | all-reduce | flops 2 | bytes 16 | tf_op jit(solution)/shard_map/psum | solution.py:37
  372.0 3.1 all-reduce.3
  375.1 18.1 %all-reduce = (f32[]{:T(128)}, f32[]{:T(128)}) all-reduce(f32[]{:T(128)} %get-tuple-element.36, f32[]{:T(128)} %get-tuple-element.37), channel_id=1, replica_groups=mesh['dp_0'=4,'dp_1'=4,'dp_2'=2,'mp'=8] {'mp'}, use_global_device_ids=true, to_apply=%region_8.0 | all-reduce | flops 2 | bytes 16 | tf_op jit(solution)/shard_map/psum | solution.py:37
  394.6 2.0 multiply_subtract_fusion
  (50 shorter events, 4.7 us)
Async XLA Ops:
  7.2 51.1 %all-gather.4.cloned.1.call-start = ((), (), s32[]{:S(2)}) async-start(), calls=%async_computation.2 | async-start | bytes 3538944 | tf_op jit(solution)/shard_map/all_gather | solution.py:109
  10.2 101.2 %all-gather.6.cloned.1.call-start = ((), (), s32[]{:S(2)}) async-start(), calls=%async_computation.3 | async-start | bytes 4866048 | tf_op jit(solution)/shard_map/all_gather | solution.py:18
  12.8 156.2 %reduce-scatter.5.cloned.1.call-start = ((), (), s32[]{:S(2)}) async-start(), calls=%async_computation.4 | async-start | bytes 3538944 | tf_op jit(solution)/shard_map/reduce_scatter | solution.py:130
  58.3 53.1 %copy-start = (bf16[1024,1536]{0,1:T(8,128)(2,1)S(1)}, bf16[1024,1536]{0,1:T(8,128)(2,1)}, u32[]{:S(2)}) copy-start(bf16[1024,1536]{0,1:T(8,128)(2,1)} %all-gather.4.cloned.1.call-done) | copy-start | bytes 9437188
  111.3 6.4 %copy-start.12 = (bf16[1536,1536]{1,0:T(8,128)(2,1)S(1)}, bf16[1536,1536]{1,0:T(8,128)(2,1)}, u32[]{:S(2)}) copy-start(bf16[1536,1536]{1,0:T(8,128)(2,1)} %all-gather.6.cloned.1.call-done) | copy-start | bytes 14155780
  115.9 1.8 copy-start.14
  122.1 48.0 %copy-start.2 = (bf16[4,256,192]{1,2,0:T(8,128)(2,1)S(1)}, bf16[4,256,192]{1,2,0:T(8,128)(2,1)}, u32[]{:S(2)}) copy-start(bf16[4,256,192]{1,2,0:T(8,128)(2,1)} %param.13) | copy-start | bytes 1179652
  122.1 48.0 %copy-start.3 = (bf16[4,256,192]{1,2,0:T(8,128)(2,1)S(1)}, bf16[4,256,192]{1,2,0:T(8,128)(2,1)}, u32[]{:S(2)}) copy-start(bf16[4,256,192]{1,2,0:T(8,128)(2,1)} %param.12) | copy-start | bytes 1179652
  122.1 48.0 %copy-start.6 = (bf16[4,256,192]{1,2,0:T(8,128)(2,1)S(1)}, bf16[4,256,192]{1,2,0:T(8,128)(2,1)}, u32[]{:S(2)}) copy-start(bf16[4,256,192]{1,2,0:T(8,128)(2,1)} %param.14) | copy-start | bytes 1179652
  122.1 48.0 %copy-start.7 = (bf16[4,256,192]{1,2,0:T(8,128)(2,1)S(1)}, bf16[4,256,192]{1,2,0:T(8,128)(2,1)}, u32[]{:S(2)}) copy-start(bf16[4,256,192]{1,2,0:T(8,128)(2,1)} %param.15) | copy-start | bytes 1179652
  122.1 95.1 %all-gather.8.cloned.1.call-start = ((), (), s32[]{:S(2)}) async-start(), calls=%async_computation.5 | async-start | bytes 3538944 | tf_op jit(solution)/shard_map/all_gather | solution.py:141
  172.5 176.6 %reduce-scatter.7.cloned.1.call-start = ((), (), s32[]{:S(2)}) async-start(), calls=%async_computation.6 | async-start | bytes 9732096 | tf_op jit(solution)/shard_map/reduce_scatter | solution.py:32
  217.2 8.1 %copy-start.13 = (bf16[1024,1536]{0,1:T(8,128)(2,1)S(1)}, bf16[1024,1536]{0,1:T(8,128)(2,1)}, u32[]{:S(2)}) copy-start(bf16[1024,1536]{0,1:T(8,128)(2,1)} %all-gather.8.cloned.1.call-done) | copy-start | bytes 9437188
  225.3 5.2 %copy-start.1 = (bf16[1024,1536]{0,1:T(8,128)(2,1)S(1)}, bf16[1024,1536]{0,1:T(8,128)(2,1)}, u32[]{:S(2)}) copy-start(bf16[1024,1536]{0,1:T(8,128)(2,1)} %all-gather.4.cloned.1.call-done) | copy-start | bytes 9437188
  247.5 147.1 %copy-start.4 = (f32[48,768]{1,0:T(8,128)S(1)}, f32[48,768]{1,0:T(8,128)}, u32[]{:S(2)}) copy-start(f32[48,768]{1,0:T(8,128)} %param.19) | copy-start | bytes 442372
  247.5 147.1 %copy-start.5 = (f32[48,768]{1,0:T(8,128)S(1)}, f32[48,768]{1,0:T(8,128)}, u32[]{:S(2)}) copy-start(f32[48,768]{1,0:T(8,128)} %param.18) | copy-start | bytes 442372
  247.5 147.1 %copy-start.8 = (f32[48,768]{1,0:T(8,128)S(1)}, f32[48,768]{1,0:T(8,128)}, u32[]{:S(2)}) copy-start(f32[48,768]{1,0:T(8,128)} %param.21) | copy-start | bytes 442372
  247.5 147.1 %copy-start.9 = (f32[48,768]{1,0:T(8,128)S(1)}, f32[48,768]{1,0:T(8,128)}, u32[]{:S(2)}) copy-start(f32[48,768]{1,0:T(8,128)} %param.23) | copy-start | bytes 442372
  247.5 147.1 %copy-start.10 = (f32[48,768]{1,0:T(8,128)S(1)}, f32[48,768]{1,0:T(8,128)}, u32[]{:S(2)}) copy-start(f32[48,768]{1,0:T(8,128)} %param.22) | copy-start | bytes 442372
  247.5 147.1 %copy-start.11 = (f32[48,768]{1,0:T(8,128)S(1)}, f32[48,768]{1,0:T(8,128)}, u32[]{:S(2)}) copy-start(f32[48,768]{1,0:T(8,128)} %param.20) | copy-start | bytes 442372
Sparse Core Ops, SparseCore 0:
  10.3 47.9 all-gather.3
  61.4 49.9 all-gather.5
  122.2 46.7 reduce-scatter.4
  172.6 44.4 all-gather.7
  247.6 101.4 reduce-scatter.6
where the time goes:
time: 405 us; the launch traced here: 404 us
  waiting for transfers between devices  289 us (71%)
  blocking collectives  41.1 us (10%)
  matrix products  25 us (6%)
  other arithmetic  18.2 us (4%)
  between operations  17.8 us (4%)
  local copies, waits for them, and re-layouts  13.2 us (3%)
    reduce_scatter x1, waiting for transfers between devices, sent_together_2(): lax.psum_scatter(both, axis, scatter_dimension=dim, tiled=True)  102 us
    all_gather x1, waiting for transfers between devices, sent_together(): result, at, outs = (lax.all_gather(both, axis, axis=dim, tiled=True), 0, [])  50.3 us
    reduce_scatter x1, waiting for transfers between devices, per_device(): lax.psum_scatter(partial_value.astype(jnp.bfloat16), 'mp', scatter_dimens...  46.7 us
    all_gather x1, waiting for transfers between devices, per_device(): gathered = lax.all_gather(noisy_rows, 'mp', axis=1, tiled=True)  45.4 us
    all_gather x1, waiting for transfers between devices, per_device(): piece = lax.all_gather(dpred, 'mp', axis=1, tiled=True)  44.4 us
    psum x4, blocking collectives, by_axis(): return functools.reduce(lax.psum, axes, shard)  41.1 us
    unnamed x31, local copies, waits for them, and re-layouts  11.5 us
  transfers between devices with their start and end apart: 5, of which 5 were waited for; matrix products, arithmetic and copies ran while one was open for 1% of the time, Pallas kernels for 0%

commit v1 on v0

--- a/solution.py
+++ b/solution.py
@@ -106,7 +106,9 @@
         clean, noise, teacher_first, teacher_second, step_index, teacher_count
     )
     noisy_rows = latent.reshape(row_count, width_local).astype(jnp.bfloat16)
-    gathered = lax.all_gather(noisy_rows, "mp", axis=1, tiled=True)
+    gathered = jnp.concatenate(
+        lax.all_to_all(jnp.stack([noisy_rows] * lax.axis_size("mp")), "mp", 0, 0), axis=1
+    )
     gathered_f = gathered.astype(jnp.float32)
     normed = (
         gathered_f * lax.rsqrt(jnp.mean(gathered_f * gathered_f, axis=1, keepdims=True) + 1e-06)

time: 405 us -> 385 us (0.951)
  waiting for transfers between devices: 289 us -> 187 us
  blocking collectives: 41.1 us -> 123 us
    all_to_all x0 -> x1, blocking collectives: none -> 81.9 us  [per_device(): lax.all_to_all(jnp.stack([noisy_rows] * lax.axis_size('mp')), 'mp', 0, 0)]
    all_gather x1, waiting for transfers between devices: 50.3 us -> 0.02 us  [sent_together(): result, at, outs = (lax.all_gather(both, axis, axis=dim, tiled=True), 0, [])]
    all_gather x1 -> x0, waiting for transfers between devices: 45.4 us -> none  [per_device(): gathered = lax.all_gather(noisy_rows, 'mp', axis=1, tiled=True)]
    reduce_scatter x1, waiting for transfers between devices: 46.7 us -> 41 us  [per_device(): lax.psum_scatter(partial_value.astype(jnp.bfloat16), 'mp', scatter_dimens...]
    unnamed x31 -> x27, local copies, waits for them, and re-layouts: 11.5 us -> 11.3 us
  transfers between devices with their start and end apart: 5 -> 4, of which waited for: 5 -> 3; matrix products, arithmetic and copies ran while one was open for 1% -> 2% of each run, Pallas kernels for 0% -> 0%
where the time goes in v1:
time: 385 us
  waiting for transfers between devices  187 us (49%)
  blocking collectives  123 us (32%)
  matrix products  22.9 us (6%)
  other arithmetic  19.3 us (5%)
  between operations  17.8 us (5%)
  local copies, waits for them, and re-layouts  14.6 us (4%)
    reduce_scatter x1, waiting for transfers between devices, sent_together_2(): lax.psum_scatter(both, axis, scatter_dimension=dim, tiled=True)  102 us
    all_to_all x1, blocking collectives, per_device(): lax.all_to_all(jnp.stack([noisy_rows] * lax.axis_size('mp')), 'mp', 0, 0)  81.9 us
    all_gather x1, waiting for transfers between devices, per_device(): piece = lax.all_gather(dpred, 'mp', axis=1, tiled=True)  44.4 us
    psum x4, blocking collectives, by_axis(): return functools.reduce(lax.psum, axes, shard)  41.1 us
    reduce_scatter x1, waiting for transfers between devices, per_device(): lax.psum_scatter(partial_value.astype(jnp.bfloat16), 'mp', scatter_dimens...  41 us
    unnamed x27, local copies, waits for them, and re-layouts  11.3 us
    dot_general x1, matrix products, per_device(): summed = jnp.dot(piece, down_full, preferred_element_type=jnp.float32)  7.96 us
  transfers between devices with their start and end apart: 4, of which 3 were waited for; matrix products, arithmetic and copies ran while one was open for 2% of the time, Pallas kernels for 0%

profile of v1, /device:TPU:2, one launch (start us, length us, event | category | flops | bytes accessed | tf_op | source)
XLA Modules:
  0.0 384.9 jit_solution(5067227110878487639)
XLA Ops:
  7.2 0.9 convert_element_type.72
  9.8 1.2 fusion.36
  11.1 1.3 fusion.24
  12.8 81.9 %all_to_all.5 = bf16[8,1024,192]{1,2,0:T(8,128)(2,1)S(1)} all-to-all(bf16[8,1024,192]{1,2,0:T(8,128)(2,1)S(1)} %stack.2), channel_id=1, replica_groups=mesh['dp_0'=4,'dp_1'=4,'dp_2'=2,'mp'=8] {'mp'}, dimensions={0} | all-to-all | bytes 6291456 | tf_op jit(solution)/shard_map/all_to_all | solution.py:110
  96.4 4.6 %fusion.4 = f32[1024,768]{1,0:T(8,128)S(1)} fusion(bf16[1024,1536]{0,1:T(8,128)(2,1)S(1)} %fusion, bf16[1536,1536]{1,0:T(8,128)(2,1)} %all-gather.3.cloned.1.call-done), kind=kOutput, calls=%fused_computation.13 | convolution fusion | flops 2415919104 | bytes 8650752 | tf_op jit(solution)/shard_map/dot_general | solution.py:123
  101.0 1.6 copy-done.11
  102.7 4.5 %multiply_convert_fusion = bf16[1024,1536]{0,1:T(8,128)(2,1)} fusion(bf16[1536,1536]{1,0:T(8,128)(2,1)S(1)} %copy-done.9, f32[1024,768]{1,0:T(8,128)S(1)} %fusion.4), kind=kOutput, calls=%fused_computation.3 | convolution fusion | flops 2426929152 | bytes 8650752 | tf_op jit(solution)/shard_map/dot_general | solution.py:127
  108.0 1.2 sin.14
  109.7 41.0 %reduce-scatter.5.cloned.1.call-done = bf16[1024,192]{0,1:T(8,128)(2,1)} async-done(((bf16[1024,1536]{0,1:T(8,128)(2,1)}), bf16[1024,192]{0,1:T(8,128)(2,1)}) %reduce-scatter.5.cloned.1.call-update) | async-done | bytes 393232 | tf_op jit(solution)/shard_map/reduce_scatter | solution.py:132
  150.7 1.1 reshape.78
  151.8 2.7 fusion.22
  155.7 44.4 %all-gather.5.cloned.1.call-done = bf16[1024,1536]{0,1:T(8,128)(2,1)} async-done(((bf16[1024,192]{0,1:T(8,128)(2,1)}), bf16[1024,1536]{0,1:T(8,128)(2,1)}) %all-gather.5.cloned.1.call-update) | async-done | bytes 3145744 | tf_op jit(solution)/shard_map/all_gather | solution.py:143
  200.1 8.0 %multiply_convert_fusion.1 = bf16[1024,768]{1,0:T(8,128)(2,1)S(1)} fusion(f32[1024,768]{1,0:T(8,128)} %copy-done.11, bf16[1024,1536]{0,1:T(8,128)(2,1)} %all-gather.5.cloned.1.call-done, bf16[1536,1536]{1,0:T(8,128)(2,1)} %all-gather.3.cloned.1.call-done), kind=kOutput, calls=%fused_computation.10 | convolution fusion | flops 2432434176 | bytes 10223616 | tf_op jit(solution)/shard_map/dot_general | solution.py:144
  208.0 2.8 convolution_multiply_fusion.1
  210.9 3.2 convolution_multiply_fusion
  214.1 4.5 %pad_maximum_fusion = f32[1536,1536]{0,1:T(8,128)} fusion(f32[1536,768]{0,1:T(8,128)S(1)} %convolution_multiply_fusion, f32[1536,768]{0,1:T(8,128)S(1)} %convolution_multiply_fusion.1), kind=kLoop, calls=%fused_computation | loop fusion | flops 2359296 | bytes 18874368 | tf_op jit(solution)/shard_map/concatenate | solution.py:30
  218.5 9.6 %copy.73 = f32[1536,1536]{1,0:T(8,128)} copy(f32[1536,1536]{0,1:T(8,128)} %pad_maximum_fusion) | data formatting | bytes 18874368
  228.2 101.6 %reduce-scatter.7.cloned.1.call-done = f32[48,1536]{1,0:T(8,128)} async-done(((f32[1536,1536]{1,0:T(8,128)}), f32[48,1536]{1,0:T(8,128)}) %reduce-scatter.7.cloned.1.call-update) | async-done | bytes 294928 | tf_op jit(solution)/shard_map/reduce_scatter | solution.py:32
  329.8 1.6 multiply_reduce_fusion.1
  332.7 9.9 %all-reduce.2 = (f32[]{:T(128)}, f32[]{:T(128)}) all-reduce(f32[]{:T(128)S(6)} %add.97, f32[]{:T(128)} %get-tuple-element.44), channel_id=1, replica_groups=mesh['dp_0'=4,'dp_1'=4,'dp_2'=2,'mp'=8] {'dp_0'}, use_global_device_ids=true, to_apply=%region_5.0 | all-reduce | flops 2 | bytes 16 | tf_op jit(solution)/shard_map/psum | solution.py:37
  342.6 10.1 %all-reduce.1 = (f32[]{:T(128)}, f32[]{:T(128)}) all-reduce(f32[]{:T(128)} %get-tuple-element.34, f32[]{:T(128)} %get-tuple-element.35), channel_id=1, replica_groups=mesh['dp_0'=4,'dp_1'=4,'dp_2'=2,'mp'=8] {'dp_1'}, use_global_device_ids=true, to_apply=%region_6.0 | all-reduce | flops 2 | bytes 16 | tf_op jit(solution)/shard_map/psum | solution.py:37
  352.7 3.1 all-reduce.3
  355.7 18.1 %all-reduce = (f32[]{:T(128)}, f32[]{:T(128)}) all-reduce(f32[]{:T(128)} %get-tuple-element.36, f32[]{:T(128)} %get-tuple-element.37), channel_id=1, replica_groups=mesh['dp_0'=4,'dp_1'=4,'dp_2'=2,'mp'=8] {'mp'}, use_global_device_ids=true, to_apply=%region_8.0 | all-reduce | flops 2 | bytes 16 | tf_op jit(solution)/shard_map/psum | solution.py:37
  375.2 2.0 multiply_subtract_fusion
  (46 shorter events, 6.4 us)
Async XLA Ops:
  7.2 89.3 %all-gather.3.cloned.1.call-start = ((), (), s32[]{:S(2)}) async-start(), calls=%async_computation.3 | async-start | bytes 4866048 | tf_op jit(solution)/shard_map/all_gather | solution.py:18
  9.8 140.9 %reduce-scatter.5.cloned.1.call-start = ((), (), s32[]{:S(2)}) async-start(), calls=%async_computation.4 | async-start | bytes 3538944 | tf_op jit(solution)/shard_map/reduce_scatter | solution.py:132
  96.4 6.2 %copy-start.9 = (bf16[1536,1536]{1,0:T(8,128)(2,1)S(1)}, bf16[1536,1536]{1,0:T(8,128)(2,1)}, u32[]{:S(2)}) copy-start(bf16[1536,1536]{1,0:T(8,128)(2,1)} %all-gather.3.cloned.1.call-done) | copy-start | bytes 14155780
  101.0 1.7 copy-start.11
  107.1 44.7 %copy-start = (bf16[4,256,192]{1,2,0:T(8,128)(2,1)S(1)}, bf16[4,256,192]{1,2,0:T(8,128)(2,1)}, u32[]{:S(2)}) copy-start(bf16[4,256,192]{1,2,0:T(8,128)(2,1)} %param.13) | copy-start | bytes 1179652
  107.2 92.9 %all-gather.5.cloned.1.call-start = ((), (), s32[]{:S(2)}) async-start(), calls=%async_computation.5 | async-start | bytes 3538944 | tf_op jit(solution)/shard_map/all_gather | solution.py:143
  107.9 1.2 copy-start.7
  150.7 3.8 copy-start.8
  155.5 174.3 %reduce-scatter.7.cloned.1.call-start = ((), (), s32[]{:S(2)}) async-start(), calls=%async_computation.6 | async-start | bytes 9732096 | tf_op jit(solution)/shard_map/reduce_scatter | solution.py:32
  208.0 2.8 copy-start.10
  208.0 2.8 copy-start.12
  228.2 147.0 %copy-start.1 = (f32[48,768]{1,0:T(8,128)S(1)}, f32[48,768]{1,0:T(8,128)}, u32[]{:S(2)}) copy-start(f32[48,768]{1,0:T(8,128)} %param.19) | copy-start | bytes 442372
  228.2 147.0 %copy-start.2 = (f32[48,768]{1,0:T(8,128)S(1)}, f32[48,768]{1,0:T(8,128)}, u32[]{:S(2)}) copy-start(f32[48,768]{1,0:T(8,128)} %param.18) | copy-start | bytes 442372
  228.2 147.0 %copy-start.3 = (f32[48,768]{1,0:T(8,128)S(1)}, f32[48,768]{1,0:T(8,128)}, u32[]{:S(2)}) copy-start(f32[48,768]{1,0:T(8,128)} %param.21) | copy-start | bytes 442372
  228.2 147.1 %copy-start.4 = (f32[48,768]{1,0:T(8,128)S(1)}, f32[48,768]{1,0:T(8,128)}, u32[]{:S(2)}) copy-start(f32[48,768]{1,0:T(8,128)} %param.23) | copy-start | bytes 442372
  228.2 147.1 %copy-start.5 = (f32[48,768]{1,0:T(8,128)S(1)}, f32[48,768]{1,0:T(8,128)}, u32[]{:S(2)}) copy-start(f32[48,768]{1,0:T(8,128)} %param.22) | copy-start | bytes 442372
  228.2 147.1 %copy-start.6 = (f32[48,768]{1,0:T(8,128)S(1)}, f32[48,768]{1,0:T(8,128)}, u32[]{:S(2)}) copy-start(f32[48,768]{1,0:T(8,128)} %param.20) | copy-start | bytes 442372
Sparse Core Ops, SparseCore 0:
  11.1 54.2 all-gather.2
  107.3 43.3 reduce-scatter.4
  155.6 44.4 all-gather.4
  228.3 101.4 reduce-scatter.6
